TPU v7x, 256 devices: a 2x2x32 block of a 4x8x32 slice. The times are simulated.
256 devices in a mesh: groups: 4 (over x, y), shard: 64 (over z, core).
Axes of the slice: x: 2, y: 2, z: 32, core: 2. Of those that a mesh axis runs over, the one named last changes fastest.
The devices are a block of a 4x8x32 slice.
Arguments:
- echoes: float32 [1, 2, 8, 512, 8192], P(None, None, 'groups', 'shard'), parts along dimension 2, may hold values from -6 to 6
- waveform: float32 [2, 8192], replicated, may hold values from -6 to 6
- doppler_taper: float32 [512], replicated, may hold values from 0.3 to 1
- cfar_guard: int32 [8], P('groups'), parts along dimension 0, may hold values from 1 to 4, as said below
- cfar_train: int32 [8], P('groups'), parts along dimension 0, may hold values from 2 to 16
- noise_floor: float32 [8], P('groups'), parts along dimension 0, may hold values from 0.5 to 2
Outputs:
- cfar_ratio: float32 [1, 8, 512, 8192], P(None, 'groups', None, 'shard'), parts along dimension 1
There are 4 independent parts, one for each index of `groups`. A program takes and returns all parts, laid end to end along the dimension named above; an argument that names none is the same for every part. Nothing has to cross between parts.
Inputs may be any that keep to these rules, and one draw needn't show every extreme that they name: In every draw some beam has cfar_guard 4 together with cfar_train 16; no beam has more of either.
All inputs are finite; a program needn't handle non-finite values.
Results may differ from a plain program's by a relative error of at most 0.000075.
Values sent between devices are 32-bit elements; how exact they have to be, the bound alone decides.
A program may use at most 64 MiB of HBM per device.

v0:
```python
import functools
import math

import jax
import jax.numpy as jnp
import numpy as np
from jax import lax
from jax.experimental import pallas as pl
from jax.experimental.pallas import tpu as pltpu
from jax.sharding import PartitionSpec as P

MESH = pl.DeviceIdType.MESH
GA = 64
GB = 128
HALO = 20
HOP = 8
F32 = jnp.float32
BF16 = jnp.bfloat16


def split_host(table):
    high = table.astype(np.float32).astype(jnp.bfloat16)
    low = (table - high.astype(np.float64)).astype(np.float32).astype(jnp.bfloat16)
    return high, low


def tables(pulses):
    a = np.arange(GA)
    n = np.arange(GB)
    c = np.concatenate([np.arange(0, GB, 2), np.arange(1, GB, 2)])
    ang_a = 2 * math.pi / GA * (np.outer(a, a) % GA)
    ang_b = 2 * math.pi / GB * (np.outer(n, c) % GB)
    ca, sa = np.cos(ang_a), np.sin(ang_a)
    cb, sb = np.cos(ang_b), np.sin(ang_b)
    fwd_a = np.block([[ca, sa], [-sa, ca]])
    inv_a = np.block([[ca, -sa], [sa, ca]])
    fwd_b = np.block([[cb, -sb], [sb, cb]])
    inv_b = np.block([[cb.T, sb.T], [-sb.T, cb.T]])

    def left(m):
        h, l = split_host(m)
        return np.concatenate([h, h, l], axis=1)

    def right(m):
        h, l = split_host(m)
        return np.concatenate([h, h, l], axis=0)

    ang_t = 2 * math.pi / (GA * GB) * (np.outer(a, n) % (GA * GB))
    radix = pulses // GA
    ang_d = 2 * math.pi / pulses * (np.outer(a, np.arange(radix)) % pulses)
    small = np.zeros((GA, GB))
    small[:, :radix] = np.cos(ang_d)
    small[:, radix : 2 * radix] = np.sin(ang_d)
    twid = np.stack([np.cos(ang_t), np.sin(ang_t), small]).astype(np.float32)
    return (
        np.stack([left(fwd_a), left(inv_a)]),
        np.stack([right(fwd_b), right(inv_b)]),
        twid,
    )


def split(x):
    high = x.astype(BF16)
    return high, (x - high.astype(F32)).astype(BF16)


def dot_left(table, values):
    high, low = split(values)
    return jnp.dot(table, jnp.concatenate([high, low, high], axis=0), preferred_element_type=F32)


def dot_right(values, table):
    high, low = split(values)
    return jnp.dot(jnp.concatenate([high, low, high], axis=1), table, preferred_element_type=F32)


def compress(rows_re, rows_im, fwd_a, inv_a, fwd_b, inv_b, tc, ts, fr, fi):
    count = len(rows_re)
    x = jnp.concatenate(
        [jnp.concatenate(rows_re, axis=1), jnp.concatenate(rows_im, axis=1)], axis=0
    )
    y = dot_left(fwd_a, x)
    parts = []
    for p in range(count):
        yr = y[:GA, p * GB : (p + 1) * GB]
        yi = y[GA:, p * GB : (p + 1) * GB]
        parts.append(jnp.concatenate([yr * tc + yi * ts, yi * tc - yr * ts], axis=1))
    z = dot_right(jnp.concatenate(parts, axis=0), fwd_b)
    parts = []
    for p in range(count):
        zr = z[p * GA : (p + 1) * GA, :GB]
        zi = z[p * GA : (p + 1) * GA, GB:]
        parts.append(jnp.concatenate([zr * fr + zi * fi, zi * fr - zr * fi], axis=1))
    v = dot_right(jnp.concatenate(parts, axis=0), inv_b)
    re, im = [], []
    for p in range(count):
        vr = v[p * GA : (p + 1) * GA, :GB]
        vi = v[p * GA : (p + 1) * GA, GB:]
        re.append(vr * tc - vi * ts)
        im.append(vr * ts + vi * tc)
    return dot_left(
        inv_a,
        jnp.concatenate([jnp.concatenate(re, axis=1), jnp.concatenate(im, axis=1)], axis=0),
    )


def butterfly8(xs):
    r = math.sqrt(0.5)

    def add(u, v):
        return u[0] + v[0], u[1] + v[1]

    def sub(u, v):
        return u[0] - v[0], u[1] - v[1]

    def dft4(q):
        s02, d02 = add(q[0], q[2]), sub(q[0], q[2])
        s13, d13 = add(q[1], q[3]), sub(q[1], q[3])
        turned = (d13[1], -d13[0])
        return [add(s02, s13), add(d02, turned), sub(s02, s13), sub(d02, turned)]

    even, odd = dft4(xs[0::2]), dft4(xs[1::2])
    o1 = ((odd[1][0] + odd[1][1]) * r, (odd[1][1] - odd[1][0]) * r)
    o2 = (odd[2][1], -odd[2][0])
    o3 = ((odd[3][1] - odd[3][0]) * r, -(odd[3][0] + odd[3][1]) * r)
    odd = [odd[0], o1, o2, o3]
    return [add(even[k], odd[k]) for k in range(4)] + [sub(even[k], odd[k]) for k in range(4)]


def doppler_power(rows_re, rows_im, fwd_a, turn):
    count = len(rows_re)
    x = jnp.concatenate(
        [jnp.concatenate(rows_re, axis=1), jnp.concatenate(rows_im, axis=1)], axis=0
    )
    y = dot_left(fwd_a, x)
    terms = []
    for l in range(count):
        yr = y[:GA, l * GB : (l + 1) * GB]
        yi = y[GA:, l * GB : (l + 1) * GB]
        if l == 0:
            terms.append((yr, yi))
        else:
            dc, ds = turn(l)
            terms.append((yr * dc + yi * ds, yi * dc - yr * ds))
    return jnp.concatenate([r * r + i * i for r, i in butterfly8(terms)], axis=0)


def filter_grid(grid):
    turned = grid.T
    top, bottom = turned[:GA], turned[GA:]
    low = lax.broadcasted_iota(jnp.int32, (GA, GB), 1) < GA
    fr = jnp.where(low, top, pltpu.roll(bottom, GA, 1))
    fi = jnp.where(low, pltpu.roll(top, GA, 1), bottom)
    return fr, fi


def bands(guard, train):
    i = lax.broadcasted_iota(jnp.int32, (GB, GB), 0)
    j = lax.broadcasted_iota(jnp.int32, (GB, GB), 1)

    def inside(d):
        return jnp.where((d > guard) & (d <= guard + train), 1.0, 0.0).astype(F32)

    own = inside(jnp.abs(i - j))
    slot = lax.rem(i, 32)
    used = jnp.where(slot < HALO, 1.0, 0.0).astype(F32)
    left = inside(j + HALO - slot) * used
    right = inside(slot + GB - j) * used
    return own, left, right


def pack(power, lo):
    rows = power.shape[0] // 4
    lane = lax.broadcasted_iota(jnp.int32, (rows, GB), 1)
    out = None
    for r in range(4):
        block = power[r * rows : (r + 1) * rows]
        shift = (32 * r - lo) % GB
        moved = pltpu.roll(block, shift, 1) if shift else block
        out = moved if out is None else jnp.where(lane >= 32 * r, moved, out)
    return out


def kernel(
    size,
    echoes,
    waveform,
    taper,
    guard,
    train,
    noise,
    tab_a,
    tab_b,
    twid,
    out,
    x_in,
    w_in,
    ta,
    tb,
    tw,
    x_rows,
    grid,
    filt,
    own,
    recv,
    land,
    dop,
    power,
    halo_out,
    halo_in,
    result,
    in_sem,
    own_sem,
    next_sem,
    recv_sem,
    land_sem,
    hs_sem,
    hr_sem,
    out_sem,
):
    chips = size // 2
    me = lax.axis_index("shard")
    chip = lax.div(me, 2)
    core = lax.rem(me, 2)
    beams = echoes.shape[2]
    pulses = echoes.shape[3]
    depth = pulses * size

    def at(offset, k):
        return lax.rem(chip + offset + chips, chips) * 2 + k

    def dev(i):
        return {"shard": i}

    partner = chip * 2 + 1 - core

    loads = {}

    def load(name, src, dst, i):
        loads[name] = pltpu.make_async_copy(src, dst, in_sem.at[i])
        loads[name].start()

    load("x0", echoes.at[0, :, 0], x_in.at[0], 0)
    load("ta", tab_a, ta, 1)
    load("tw", twid, tw, 2)
    load("tb", tab_b, tb, 3)
    load("w", waveform, w_in, 4)
    for b in range(1, beams):
        load(f"x{b}", echoes.at[0, :, b], x_in.at[b], 4 + b)

    barrier = pltpu.get_barrier_semaphore()
    peers = [(d, k) for d in range(-HOP, HOP + 1) for k in (0, 1) if d]
    for d, k in peers:
        pl.semaphore_signal(barrier, inc=1, device_id=dev(at(d, k)), device_id_type=MESH)
    pl.semaphore_signal(barrier, inc=1, device_id=dev(partner), device_id_type=MESH)

    def range_compress(b):
        loads[f"x{b}"].wait()
        for ri in range(2):
            for j in range(GA):
                x_rows[ri, j * pulses : (j + 1) * pulses, :] = x_in[b, ri, :, j * GB : (j + 1) * GB]
        if b == 0:
            loads["w"].wait()
            for ri in range(2):
                for j in range(GA):
                    grid[ri * GA + j : ri * GA + j + 1, :] = w_in[ri : ri + 1, j * GB : (j + 1) * GB]
            fr, fi = filter_grid(grid[...])
            filt[0] = fr
            filt[1] = fi
            for name in ("ta", "tw", "tb"):
                loads[name].wait()
        rows = [
            [x_rows[ri, pl.ds(p, GA, stride=pulses), :] for p in range(pulses)] for ri in range(2)
        ]
        done = compress(
            rows[0], rows[1], ta[0], ta[1], tb[0], tb[1], tw[0], tw[1], filt[0], filt[1]
        )
        scale = 1.0 / (GA * GB * math.sqrt(depth))
        for p in range(pulses):
            weight = taper[me * pulses + p] * scale
            for ri in range(2):
                own[b, ri, pl.ds(p, GA, stride=pulses), :] = (
                    done[ri * GA : (ri + 1) * GA, p * GB : (p + 1) * GB] * weight
                )
        mine = pl.ds(pl.multiple_of(me * pulses, pulses), pulses)
        recv[b, :, mine, :] = own[b, :, mine, :]

    def rows_of(i, n=1):
        return pl.ds(pl.multiple_of(i * pulses, pulses), n * pulses)

    def first_leg(b, side, e):
        step = 1 - 2 * side
        far = at(step * (HOP + e), 0)
        to = dev(at(step * HOP, core))
        if e == HOP:
            src = own.at[b, :, rows_of(far + side)]
            dst = land.at[b, side, e - 1, :, pl.ds(side * pulses, pulses)]
        else:
            src = own.at[b, :, rows_of(far, 2)]
            dst = land.at[b, side, e - 1]
        return pltpu.make_async_remote_copy(
            src_ref=src,
            dst_ref=dst,
            send_sem=own_sem.at[b],
            recv_sem=land_sem.at[b, side, e - 1],
            device_id=to,
            device_id_type=MESH,
        )

    def direct(b, to):
        return pltpu.make_async_remote_copy(
            src_ref=own.at[b, :, rows_of(to)],
            dst_ref=recv.at[b, :, rows_of(me)],
            send_sem=own_sem.at[b],
            recv_sem=recv_sem.at[b],
            device_id=dev(to),
            device_id_type=MESH,
        )

    def second_leg(b, side, e, k):
        step = 1 - 2 * side
        src = at(-step * HOP, core)
        return pltpu.make_async_remote_copy(
            src_ref=land.at[b, side, e - 1, :, pl.ds(k * pulses, pulses)],
            dst_ref=recv.at[b, :, rows_of(src)],
            send_sem=next_sem.at[b],
            recv_sem=recv_sem.at[b],
            device_id=dev(at(step * e, k)),
            device_id_type=MESH,
        )

    def start_first(b):
        for e in range(HOP, 0, -1):
            for side in range(2):
                first_leg(b, side, e).start()

    def start_near(b):
        for e in range(HOP, 0, -1):
            for k in range(2):
                for side in range(2):
                    direct(b, at((1 - 2 * side) * e, k)).start()
        direct(b, partner).start()

    def start_second(b):
        for e in range(HOP, 0, -1):
            for side in range(2):
                first_leg(b, side, e).wait_recv()
                for k in (side,) if e == HOP else (0, 1):
                    second_leg(b, side, e, k).start()

    def wait_blocks(sem, n):
        ref = own.at[0, :, pl.ds(0, n * pulses)]
        pltpu.make_async_copy(ref, ref, sem).wait()

    def halo_copy(b, side):
        to = lax.rem(me + (1 if side else size - 1), size)
        return pltpu.make_async_remote_copy(
            src_ref=halo_out.at[b, side],
            dst_ref=halo_in.at[b, 1 - side],
            send_sem=hs_sem.at[b, side],
            recv_sem=hr_sem.at[b, 1 - side],
            device_id=dev(to),
            device_id_type=MESH,
        )

    def doppler(b):
        rows = [
            [recv[b, ri, pl.ds(l, size, stride=pulses), :] for l in range(pulses)] for ri in range(2)
        ]
        value = doppler_power(
            rows[0], rows[1], ta[0], lambda l: (dop[0, :, l * GB : (l + 1) * GB], dop[1, :, l * GB : (l + 1) * GB])
        )
        halo_out[b, 0] = pack(value, 0)
        halo_out[b, 1] = pack(value, GB - HALO)
        power[b] = value
        for side in range(2):
            halo_copy(b, side).start()

    def cfar(b):
        own_band, left_band, right_band = bands(guard[b], train[b])
        cells = power[b]
        high, low = split(cells)
        band = own_band.astype(BF16)
        total = jnp.dot(
            jnp.concatenate([high, low], axis=1),
            jnp.concatenate([band, band], axis=0),
            preferred_element_type=F32,
        )
        slot = lax.div(lax.broadcasted_iota(jnp.int32, (GB, GB), 0), 32)
        rows = depth // 4
        for side in range(2):
            halo_copy(b, side).wait_send()
            halo_copy(b, 1 - side).wait_recv()
        left = jnp.where(me > 0, halo_in[b, 0], 0.0)
        right = jnp.where(me < size - 1, halo_in[b, 1], 0.0)
        lh, ll = split(left)
        rh, rl = split(right)
        edges = jnp.concatenate([lh, ll, rh, rl], axis=1)
        floor = noise[b]
        inverse = 1.0 / (2.0 * train[b].astype(F32))
        for r in range(4):
            here = slot == r
            lb = jnp.where(here, left_band, 0.0).astype(BF16)
            rb = jnp.where(here, right_band, 0.0).astype(BF16)
            more = jnp.dot(
                edges, jnp.concatenate([lb, lb, rb, rb], axis=0), preferred_element_type=F32
            )
            window = total[r * rows : (r + 1) * rows] + more
            result[b, r * rows : (r + 1) * rows, :] = cells[r * rows : (r + 1) * rows] / (
                floor + window * inverse
            )
        pltpu.make_async_copy(result.at[b], out.at[0, b], out_sem.at[b]).start()

    range_compress(0)
    pl.semaphore_wait(barrier, len(peers) + 1)
    start_first(0)
    start_near(0)
    for b in range(1, beams):
        range_compress(b)
    for l in range(pulses):
        for i in range(2):
            col = i * pulses + l
            dop[i, :, l * GB : (l + 1) * GB] = jnp.broadcast_to(tw[2, :, col : col + 1], (GA, GB))
    for b in range(beams):
        start_second(b)
        if b + 1 < beams:
            start_first(b + 1)
            start_near(b + 1)
        if b > 0:
            cfar(b - 1)
        wait_blocks(recv_sem.at[b], size - 1)
        doppler(b)
    cfar(beams - 1)
    for b in range(beams):
        wait_blocks(own_sem.at[b], size - 1)
        wait_blocks(next_sem.at[b], 4 * HOP - 2)
        pltpu.make_async_copy(result.at[b], out.at[0, b], out_sem.at[b]).wait()


def solution(mesh):
    size = mesh.shape["shard"]

    def step(echoes, waveform, taper, guard, train, noise):
        _, _, beams, pulses, gates = echoes.shape
        depth = pulses * size
        tab_a, tab_b, twid = tables(depth)
        hbm = pl.BlockSpec(memory_space=pl.ANY)
        smem = pl.BlockSpec(memory_space=pltpu.SMEM)
        vmem = pltpu.VMEM
        dma = pltpu.SemaphoreType.DMA
        return pl.pallas_call(
            functools.partial(kernel, size),
            out_shape=jax.ShapeDtypeStruct((1, beams, depth, GB), F32),
            in_specs=[hbm, hbm, smem, smem, smem, smem, hbm, hbm, hbm],
            out_specs=hbm,
            scratch_shapes=[
                vmem((beams, 2, pulses, gates), F32),
                vmem((2, gates), F32),
                vmem(tab_a.shape, BF16),
                vmem(tab_b.shape, BF16),
                vmem(twid.shape, F32),
                vmem((2, GA * pulses, GB), F32),
                vmem((GB, GB), F32),
                vmem((2, GA, GB), F32),
                vmem((beams, 2, depth, GB), F32),
                vmem((beams, 2, depth, GB), F32),
                vmem((beams, 2, HOP, 2, 2 * pulses, GB), F32),
                vmem((2, GA, pulses * GB), F32),
                vmem((beams, depth, GB), F32),
                vmem((beams, 2, depth // 4, GB), F32),
                vmem((beams, 2, depth // 4, GB), F32),
                vmem((beams, depth, GB), F32),
                dma((4 + beams,)),
                dma((beams,)),
                dma((beams,)),
                dma((beams,)),
                dma((beams, 2, HOP)),
                dma((beams, 2)),
                dma((beams, 2)),
                dma((beams,)),
            ],
            compiler_params=pltpu.CompilerParams(
                collective_id=0, has_side_effects=True, vmem_limit_bytes=56 * 2**20
            ),
            name="pulse_doppler",
        )(echoes, waveform, taper, guard, train, noise, jnp.asarray(tab_a), jnp.asarray(tab_b), jnp.asarray(twid))

    in_specs = (
        P(None, None, "groups", "shard", None),
        P(),
        P(),
        P("groups"),
        P("groups"),
        P("groups"),
    )
    out_specs = P(None, "groups", None, "shard")
    return jax.shard_map(step, mesh=mesh, in_specs=in_specs, out_specs=out_specs, check_vma=False)
```

profile of v0, /device:TPU:37, one launch (start us, length us, event | category | flops | bytes accessed | tf_op | source)
XLA Modules:
  0.0 129.7 jit_solution(3368014559663312114)
XLA Ops:
  0.0 127.8 %pulse_doppler.1 = f32[1,2,512,128]{3,2,1,0:T(8,128)} custom-call(f32[1,2,2,8,8192]{4,3,2,1,0:T(8,128)} %echoes.1, f32[2,8192]{1,0:T(2,128)} %waveform.1, f32[512]{0:T(512)} %taper.1, s32[2]{0:T(128)} %guard.1, s32[2]{0:T(128)} %train.1, f32[2]{0:T(128)} %noise.1, bf16[2,128,384]{2,1,0:T(8,128)(2,1)} %constant.6.clone.tab_a, ...), custom_call_target="tpu_custom_call" | custom-call | tf_op jit(solution)/shard_map/pulse_doppler/pallas_call | solution.py:451
  127.8 1.9 %copy.11 = f32[1,2,512,128]{3,2,1,0:T(8,128)} copy(f32[1,2,512,128]{3,2,1,0:T(8,128)} %pulse_doppler.1) | data formatting | bytes 1048576
where the time goes:
time: 130 us
  Pallas kernels  128 us (98%)
  local copies, waits for them, and re-layouts  1.87 us (1%)
    pallas_call x1, Pallas kernels, step(): pl.pallas_call(functools.partial(kernel, size), out_shape=jax.ShapeDtypeS...  128 us

commit v1 on v0

--- a/solution.py
+++ b/solution.py
@@ -203,7 +203,6 @@
     filt,
     own,
     recv,
-    land,
     dop,
     power,
     halo_out,
@@ -211,9 +210,8 @@
     result,
     in_sem,
     own_sem,
-    next_sem,
     recv_sem,
-    land_sem,
+    ready,
     hs_sem,
     hr_sem,
     out_sem,
@@ -288,25 +286,6 @@
     def rows_of(i, n=1):
         return pl.ds(pl.multiple_of(i * pulses, pulses), n * pulses)
 
-    def first_leg(b, side, e):
-        step = 1 - 2 * side
-        far = at(step * (HOP + e), 0)
-        to = dev(at(step * HOP, core))
-        if e == HOP:
-            src = own.at[b, :, rows_of(far + side)]
-            dst = land.at[b, side, e - 1, :, pl.ds(side * pulses, pulses)]
-        else:
-            src = own.at[b, :, rows_of(far, 2)]
-            dst = land.at[b, side, e - 1]
-        return pltpu.make_async_remote_copy(
-            src_ref=src,
-            dst_ref=dst,
-            send_sem=own_sem.at[b],
-            recv_sem=land_sem.at[b, side, e - 1],
-            device_id=to,
-            device_id_type=MESH,
-        )
-
     def direct(b, to):
         return pltpu.make_async_remote_copy(
             src_ref=own.at[b, :, rows_of(to)],
@@ -317,36 +296,40 @@
             device_id_type=MESH,
         )
 
-    def second_leg(b, side, e, k):
-        step = 1 - 2 * side
-        src = at(-step * HOP, core)
-        return pltpu.make_async_remote_copy(
-            src_ref=land.at[b, side, e - 1, :, pl.ds(k * pulses, pulses)],
-            dst_ref=recv.at[b, :, rows_of(src)],
-            send_sem=next_sem.at[b],
-            recv_sem=recv_sem.at[b],
-            device_id=dev(at(step * e, k)),
-            device_id_type=MESH,
-        )
-
-    def start_first(b):
-        for e in range(HOP, 0, -1):
-            for side in range(2):
-                first_leg(b, side, e).start()
-
     def start_near(b):
-        for e in range(HOP, 0, -1):
+        direct(b, partner).start()
+        for e in range(1, HOP + 1):
             for k in range(2):
-                for side in range(2):
-                    direct(b, at((1 - 2 * side) * e, k)).start()
+                for step in (1, -1):
+                    direct(b, at(step * e, k)).start()
+
+    def start_far(b):
+        for e in range(HOP + 1, chips // 2):
+            for k in range(2):
+                for step in (1, -1):
+                    direct(b, at(step * e, k)).start()
+        for k in range(2):
+            direct(b, at(chips // 2, k)).start()
+
+    def start_by_place(b):
+        half = chips // 2
+        late = chip >= half
+
+        def opposite():
+            for k in range(2):
+                direct(b, at(half, k)).start()
+
         direct(b, partner).start()
-
-    def start_second(b):
-        for e in range(HOP, 0, -1):
-            for side in range(2):
-                first_leg(b, side, e).wait_recv()
-                for k in (side,) if e == HOP else (0, 1):
-                    second_leg(b, side, e, k).start()
+        pl.when(late)(opposite)
+        up = jnp.where(late, chips - chip, 1)
+        down = jnp.minimum(chip, half - 1)
+        for i in range(half - 1):
+            forward = lax.rem(up - 1 + i, half - 1) + 1
+            backward = lax.rem(down - 1 - i + 2 * (half - 1), half - 1) + 1
+            for k in range(2):
+                direct(b, at(forward, k)).start()
+                direct(b, at(-backward, k)).start()
+        pl.when(jnp.logical_not(late))(opposite)
 
     def wait_blocks(sem, n):
         ref = own.at[0, :, pl.ds(0, n * pulses)]
@@ -413,27 +396,25 @@
 
     range_compress(0)
     pl.semaphore_wait(barrier, len(peers) + 1)
-    start_first(0)
+    for step in (1, -1):
+        pl.semaphore_signal(ready, inc=1, device_id=dev(at(step * HOP, core)), device_id_type=MESH)
     start_near(0)
     for b in range(1, beams):
         range_compress(b)
+    pl.semaphore_wait(ready, 2)
+    start_far(0)
+    for b in range(1, beams):
+        start_by_place(b)
     for l in range(pulses):
         for i in range(2):
             col = i * pulses + l
             dop[i, :, l * GB : (l + 1) * GB] = jnp.broadcast_to(tw[2, :, col : col + 1], (GA, GB))
     for b in range(beams):
-        start_second(b)
-        if b + 1 < beams:
-            start_first(b + 1)
-            start_near(b + 1)
-        if b > 0:
-            cfar(b - 1)
         wait_blocks(recv_sem.at[b], size - 1)
         doppler(b)
-    cfar(beams - 1)
+        cfar(b)
     for b in range(beams):
         wait_blocks(own_sem.at[b], size - 1)
-        wait_blocks(next_sem.at[b], 4 * HOP - 2)
         pltpu.make_async_copy(result.at[b], out.at[0, b], out_sem.at[b]).wait()
 
 
@@ -464,7 +445,6 @@
                 vmem((2, GA, GB), F32),
                 vmem((beams, 2, depth, GB), F32),
                 vmem((beams, 2, depth, GB), F32),
-                vmem((beams, 2, HOP, 2, 2 * pulses, GB), F32),
                 vmem((2, GA, pulses * GB), F32),
                 vmem((beams, depth, GB), F32),
                 vmem((beams, 2, depth // 4, GB), F32),
@@ -473,8 +453,7 @@
                 dma((4 + beams,)),
                 dma((beams,)),
                 dma((beams,)),
-                dma((beams,)),
-                dma((beams, 2, HOP)),
+                pltpu.SemaphoreType.REGULAR,
                 dma((beams, 2)),
                 dma((beams, 2)),
                 dma((beams,)),

time: 130 us -> 135 us (1.038)
  the two profiles are of different devices: /device:TPU:37 before, /device:TPU:46 now
where the time goes in v1:
time: 135 us
  Pallas kernels  133 us (99%)
  local copies, waits for them, and re-layouts  1.87 us (1%)
    pallas_call x1, Pallas kernels, step(): pl.pallas_call(functools.partial(kernel, size), out_shape=jax.ShapeDtypeS...  133 us

profile of v1, /device:TPU:46, one launch (start us, length us, event | category | flops | bytes accessed | tf_op | source)
XLA Modules:
  0.0 134.9 jit_solution(6152108769564065430)
XLA Ops:
  0.0 133.1 %pulse_doppler.1 = f32[1,2,512,128]{3,2,1,0:T(8,128)} custom-call(f32[1,2,2,8,8192]{4,3,2,1,0:T(8,128)} %echoes.1, f32[2,8192]{1,0:T(2,128)} %waveform.1, f32[512]{0:T(512)} %taper.1, s32[2]{0:T(128)} %guard.1, s32[2]{0:T(128)} %train.1, f32[2]{0:T(128)} %noise.1, bf16[2,128,384]{2,1,0:T(8,128)(2,1)} %constant.6.clone.tab_a, ...), custom_call_target="tpu_custom_call" | custom-call | tf_op jit(solution)/shard_map/pulse_doppler/pallas_call | solution.py:432
  133.1 1.9 %copy.11 = f32[1,2,512,128]{3,2,1,0:T(8,128)} copy(f32[1,2,512,128]{3,2,1,0:T(8,128)} %pulse_doppler.1) | data formatting | bytes 1048576

commit v2 on v1

--- a/solution.py
+++ b/solution.py
@@ -207,14 +207,12 @@
     power,
     halo_out,
     halo_in,
-    result,
     in_sem,
     own_sem,
     recv_sem,
     ready,
     hs_sem,
     hr_sem,
-    out_sem,
 ):
     chips = size // 2
     me = lax.axis_index("shard")
@@ -296,44 +294,51 @@
             device_id_type=MESH,
         )
 
-    def start_near(b):
-        direct(b, partner).start()
-        for e in range(1, HOP + 1):
+    def start_by_place(b, lo, hi):
+        half = chips // 2
+
+        def both(offset):
             for k in range(2):
-                for step in (1, -1):
-                    direct(b, at(step * e, k)).start()
-
-    def start_far(b):
-        for e in range(HOP + 1, chips // 2):
-            for k in range(2):
-                for step in (1, -1):
-                    direct(b, at(step * e, k)).start()
-        for k in range(2):
-            direct(b, at(chips // 2, k)).start()
-
-    def start_by_place(b):
-        half = chips // 2
-        late = chip >= half
-
-        def opposite():
-            for k in range(2):
-                direct(b, at(half, k)).start()
-
-        direct(b, partner).start()
-        pl.when(late)(opposite)
-        up = jnp.where(late, chips - chip, 1)
-        down = jnp.minimum(chip, half - 1)
-        for i in range(half - 1):
-            forward = lax.rem(up - 1 + i, half - 1) + 1
-            backward = lax.rem(down - 1 - i + 2 * (half - 1), half - 1) + 1
-            for k in range(2):
-                direct(b, at(forward, k)).start()
-                direct(b, at(-backward, k)).start()
-        pl.when(jnp.logical_not(late))(opposite)
+                direct(b, at(offset, k)).start()
+
+        def when(condition, offset):
+            pl.when(condition)(lambda: both(offset))
+
+        def early():
+            for m in range(1, half):
+                if lo <= m <= hi:
+                    both(m)
+                if lo <= half - m <= hi:
+                    when(half - m <= chip, m - half)
+            for m in range(half - 1, 0, -1):
+                if lo <= m <= hi:
+                    when(m > chip, -m)
+            if hi >= half:
+                both(half)
+
+        def late():
+            if hi >= half:
+                both(half)
+            for place in range(half):
+                up = chips - chip + place
+                when((up >= lo) & (up <= min(hi, half - 1)), up)
+                down = chip - place
+                when((down >= lo) & (down <= min(hi, half - 1)), -down)
+            for m in range(half - 1, 0, -1):
+                if lo <= m <= hi:
+                    when(chip + m < chips, m)
+                    when(chip - m >= half, -m)
+
+        if lo == 1:
+            direct(b, partner).start()
+        pl.when(chip < half)(early)
+        pl.when(chip >= half)(late)
 
     def wait_blocks(sem, n):
         ref = own.at[0, :, pl.ds(0, n * pulses)]
         pltpu.make_async_copy(ref, ref, sem).wait()
+
+    inner = (me > 0, me < size - 1)
 
     def halo_copy(b, side):
         to = lax.rem(me + (1 if side else size - 1), size)
@@ -357,7 +362,7 @@
         halo_out[b, 1] = pack(value, GB - HALO)
         power[b] = value
         for side in range(2):
-            halo_copy(b, side).start()
+            pl.when(inner[side])(halo_copy(b, side).start)
 
     def cfar(b):
         own_band, left_band, right_band = bands(guard[b], train[b])
@@ -372,10 +377,17 @@
         slot = lax.div(lax.broadcasted_iota(jnp.int32, (GB, GB), 0), 32)
         rows = depth // 4
         for side in range(2):
-            halo_copy(b, side).wait_send()
-            halo_copy(b, 1 - side).wait_recv()
-        left = jnp.where(me > 0, halo_in[b, 0], 0.0)
-        right = jnp.where(me < size - 1, halo_in[b, 1], 0.0)
+
+            def arrived():
+                halo_copy(b, side).wait_send()
+                halo_copy(b, 1 - side).wait_recv()
+
+            def outside():
+                halo_in[b, side] = jnp.zeros_like(halo_in[b, side])
+
+            pl.when(inner[side])(arrived)
+            pl.when(jnp.logical_not(inner[side]))(outside)
+        left, right = halo_in[b, 0], halo_in[b, 1]
         lh, ll = split(left)
         rh, rl = split(right)
         edges = jnp.concatenate([lh, ll, rh, rl], axis=1)
@@ -389,22 +401,21 @@
                 edges, jnp.concatenate([lb, lb, rb, rb], axis=0), preferred_element_type=F32
             )
             window = total[r * rows : (r + 1) * rows] + more
-            result[b, r * rows : (r + 1) * rows, :] = cells[r * rows : (r + 1) * rows] / (
+            out[0, b, r * rows : (r + 1) * rows, :] = cells[r * rows : (r + 1) * rows] / (
                 floor + window * inverse
             )
-        pltpu.make_async_copy(result.at[b], out.at[0, b], out_sem.at[b]).start()
 
     range_compress(0)
     pl.semaphore_wait(barrier, len(peers) + 1)
     for step in (1, -1):
         pl.semaphore_signal(ready, inc=1, device_id=dev(at(step * HOP, core)), device_id_type=MESH)
-    start_near(0)
+    start_by_place(0, 1, HOP)
     for b in range(1, beams):
         range_compress(b)
     pl.semaphore_wait(ready, 2)
-    start_far(0)
+    start_by_place(0, HOP + 1, chips // 2)
     for b in range(1, beams):
-        start_by_place(b)
+        start_by_place(b, 1, chips // 2)
     for l in range(pulses):
         for i in range(2):
             col = i * pulses + l
@@ -415,7 +426,6 @@
         cfar(b)
     for b in range(beams):
         wait_blocks(own_sem.at[b], size - 1)
-        pltpu.make_async_copy(result.at[b], out.at[0, b], out_sem.at[b]).wait()
 
 
 def solution(mesh):
@@ -433,7 +443,7 @@
             functools.partial(kernel, size),
             out_shape=jax.ShapeDtypeStruct((1, beams, depth, GB), F32),
             in_specs=[hbm, hbm, smem, smem, smem, smem, hbm, hbm, hbm],
-            out_specs=hbm,
+            out_specs=pl.BlockSpec(memory_space=vmem),
             scratch_shapes=[
                 vmem((beams, 2, pulses, gates), F32),
                 vmem((2, gates), F32),
@@ -449,14 +459,12 @@
                 vmem((beams, depth, GB), F32),
                 vmem((beams, 2, depth // 4, GB), F32),
                 vmem((beams, 2, depth // 4, GB), F32),
-                vmem((beams, depth, GB), F32),
                 dma((4 + beams,)),
                 dma((beams,)),
                 dma((beams,)),
                 pltpu.SemaphoreType.REGULAR,
                 dma((beams, 2)),
                 dma((beams, 2)),
-                dma((beams,)),
             ],
             compiler_params=pltpu.CompilerParams(
                 collective_id=0, has_side_effects=True, vmem_limit_bytes=56 * 2**20

time: 135 us -> 124 us (0.919)
  the two profiles are of different devices: /device:TPU:46 before, /device:TPU:37 now
where the time goes in v2:
time: 124 us
  Pallas kernels  122 us (98%)
  local copies, waits for them, and re-layouts  1.87 us (2%)
    pallas_call x1, Pallas kernels, step(): pl.pallas_call(functools.partial(kernel, size), out_shape=jax.ShapeDtypeS...  122 us

profile of v2, /device:TPU:37, one launch (start us, length us, event | category | flops | bytes accessed | tf_op | source)
XLA Modules:
  0.0 124.1 jit_solution(6312294041433828286)
XLA Ops:
  0.0 122.2 %pulse_doppler.1 = f32[1,2,512,128]{3,2,1,0:T(8,128)} custom-call(f32[1,2,2,8,8192]{4,3,2,1,0:T(8,128)} %echoes.1, f32[2,8192]{1,0:T(2,128)} %waveform.1, f32[512]{0:T(512)} %taper.1, s32[2]{0:T(128)} %guard.1, s32[2]{0:T(128)} %train.1, f32[2]{0:T(128)} %noise.1, bf16[2,128,384]{2,1,0:T(8,128)(2,1)} %constant.6.clone.tab_a, ...), custom_call_target="tpu_custom_call" | custom-call | tf_op jit(solution)/shard_map/pulse_doppler/pallas_call | solution.py:442
  122.3 1.9 %copy.11 = f32[1,2,512,128]{3,2,1,0:T(8,128)} copy(f32[1,2,512,128]{3,2,1,0:T(8,128)} %pulse_doppler.1) | data formatting | bytes 1048576

commit v3 on v2

--- a/solution.py
+++ b/solution.py
@@ -14,6 +14,7 @@
 GB = 128
 HALO = 20
 HOP = 8
+NEAR = 2
 F32 = jnp.float32
 BF16 = jnp.bfloat16
 
@@ -205,6 +206,7 @@
     recv,
     dop,
     power,
+    window,
     halo_out,
     halo_in,
     in_sem,
@@ -244,11 +246,23 @@
     for b in range(1, beams):
         load(f"x{b}", echoes.at[0, :, b], x_in.at[b], 4 + b)
 
+    half = chips // 2
+    first_half = chip < half
+
     barrier = pltpu.get_barrier_semaphore()
-    peers = [(d, k) for d in range(-HOP, HOP + 1) for k in (0, 1) if d]
-    for d, k in peers:
-        pl.semaphore_signal(barrier, inc=1, device_id=dev(at(d, k)), device_id_type=MESH)
+
+    def greet(offsets):
+        for d in offsets:
+            for k in range(2):
+                pl.semaphore_signal(barrier, inc=1, device_id=dev(at(d, k)), device_id_type=MESH)
+
+    wide = [d for d in range(-HOP, HOP + 1) if abs(d) > NEAR]
     pl.semaphore_signal(barrier, inc=1, device_id=dev(partner), device_id_type=MESH)
+    greet([d for d in range(-NEAR, NEAR + 1) if d])
+    pl.when(first_half)(lambda: greet(wide))
+    greeters = 1 + 4 * NEAR
+    for d in wide:
+        greeters += jnp.where(lax.rem(chip + d + chips, chips) < half, 2, 0)
 
     def range_compress(b):
         loads[f"x{b}"].wait()
@@ -294,9 +308,7 @@
             device_id_type=MESH,
         )
 
-    def start_by_place(b, lo, hi):
-        half = chips // 2
-
+    def start_by_place(b, lo, hi, to=None):
         def both(offset):
             for k in range(2):
                 direct(b, at(offset, k)).start()
@@ -307,11 +319,16 @@
         def early():
             for m in range(1, half):
                 if lo <= m <= hi:
-                    both(m)
-                if lo <= half - m <= hi:
+                    if to is None:
+                        both(m)
+                    elif to == 0:
+                        when(chip + m < half, m)
+                    else:
+                        when(chip + m >= half, m)
+                if lo <= half - m <= hi and to != 1:
                     when(half - m <= chip, m - half)
             for m in range(half - 1, 0, -1):
-                if lo <= m <= hi:
+                if lo <= m <= hi and to != 0:
                     when(m > chip, -m)
             if hi >= half:
                 both(half)
@@ -319,20 +336,26 @@
         def late():
             if hi >= half:
                 both(half)
-            for place in range(half):
-                up = chips - chip + place
-                when((up >= lo) & (up <= min(hi, half - 1)), up)
-                down = chip - place
-                when((down >= lo) & (down <= min(hi, half - 1)), -down)
-            for m in range(half - 1, 0, -1):
-                if lo <= m <= hi:
-                    when(chip + m < chips, m)
-                    when(chip - m >= half, -m)
-
-        if lo == 1:
-            direct(b, partner).start()
-        pl.when(chip < half)(early)
-        pl.when(chip >= half)(late)
+            if to != 1:
+                for place in range(half):
+                    up = chips - chip + place
+                    when((up >= lo) & (up <= min(hi, half - 1)), up)
+                    down = chip - place
+                    when((down >= lo) & (down <= min(hi, half - 1)), -down)
+            if to != 0:
+                for m in range(half - 1, 0, -1):
+                    if lo <= m <= hi:
+                        when(chip + m < chips, m)
+                        when(chip - m >= half, -m)
+
+        pl.when(first_half)(early)
+        pl.when(jnp.logical_not(first_half))(late)
+
+    def tell(step):
+        for sign in (1, -1):
+            pl.semaphore_signal(
+                ready.at[step], inc=1, device_id=dev(at(sign * (NEAR << step), core)), device_id_type=MESH
+            )
 
     def wait_blocks(sem, n):
         ref = own.at[0, :, pl.ds(0, n * pulses)]
@@ -364,16 +387,17 @@
         for side in range(2):
             pl.when(inner[side])(halo_copy(b, side).start)
 
-    def cfar(b):
-        own_band, left_band, right_band = bands(guard[b], train[b])
-        cells = power[b]
-        high, low = split(cells)
-        band = own_band.astype(BF16)
-        total = jnp.dot(
+    def cfar_inside(b):
+        high, low = split(power[b])
+        band = bands(guard[b], train[b])[0].astype(BF16)
+        window[b] = jnp.dot(
             jnp.concatenate([high, low], axis=1),
             jnp.concatenate([band, band], axis=0),
             preferred_element_type=F32,
         )
+
+    def cfar(b):
+        _, left_band, right_band = bands(guard[b], train[b])
         slot = lax.div(lax.broadcasted_iota(jnp.int32, (GB, GB), 0), 32)
         rows = depth // 4
         for side in range(2):
@@ -394,28 +418,33 @@
         floor = noise[b]
         inverse = 1.0 / (2.0 * train[b].astype(F32))
         for r in range(4):
-            here = slot == r
-            lb = jnp.where(here, left_band, 0.0).astype(BF16)
-            rb = jnp.where(here, right_band, 0.0).astype(BF16)
+            lb = jnp.where(slot == r, left_band, 0.0).astype(BF16)
+            rb = jnp.where(slot == r, right_band, 0.0).astype(BF16)
             more = jnp.dot(
                 edges, jnp.concatenate([lb, lb, rb, rb], axis=0), preferred_element_type=F32
             )
-            window = total[r * rows : (r + 1) * rows] + more
-            out[0, b, r * rows : (r + 1) * rows, :] = cells[r * rows : (r + 1) * rows] / (
-                floor + window * inverse
-            )
+            here = slice(r * rows, (r + 1) * rows)
+            out[0, b, here, :] = power[b, here, :] / (floor + (window[b, here, :] + more) * inverse)
 
     range_compress(0)
-    pl.semaphore_wait(barrier, len(peers) + 1)
-    for step in (1, -1):
-        pl.semaphore_signal(ready, inc=1, device_id=dev(at(step * HOP, core)), device_id_type=MESH)
-    start_by_place(0, 1, HOP)
+    pl.semaphore_wait(barrier, greeters)
+    tell(0)
+    direct(0, partner).start()
+    start_by_place(0, 1, NEAR)
+    start_by_place(0, NEAR + 1, HOP, 0)
     for b in range(1, beams):
         range_compress(b)
-    pl.semaphore_wait(ready, 2)
-    start_by_place(0, HOP + 1, chips // 2)
+    pl.semaphore_wait(ready.at[0], 2)
+    tell(1)
+    start_by_place(0, NEAR + 1, 2 * NEAR, 1)
+    pl.semaphore_wait(ready.at[1], 2)
+    tell(2)
+    start_by_place(0, 2 * NEAR + 1, HOP, 1)
+    pl.semaphore_wait(ready.at[2], 2)
+    start_by_place(0, HOP + 1, half)
     for b in range(1, beams):
-        start_by_place(b, 1, chips // 2)
+        direct(b, partner).start()
+        start_by_place(b, 1, half)
     for l in range(pulses):
         for i in range(2):
             col = i * pulses + l
@@ -423,6 +452,8 @@
     for b in range(beams):
         wait_blocks(recv_sem.at[b], size - 1)
         doppler(b)
+        cfar_inside(b)
+    for b in range(beams):
         cfar(b)
     for b in range(beams):
         wait_blocks(own_sem.at[b], size - 1)
@@ -457,12 +488,13 @@
                 vmem((beams, 2, depth, GB), F32),
                 vmem((2, GA, pulses * GB), F32),
                 vmem((beams, depth, GB), F32),
+                vmem((beams, depth, GB), F32),
                 vmem((beams, 2, depth // 4, GB), F32),
                 vmem((beams, 2, depth // 4, GB), F32),
                 dma((4 + beams,)),
                 dma((beams,)),
                 dma((beams,)),
-                pltpu.SemaphoreType.REGULAR,
+                pltpu.SemaphoreType.REGULAR((3,)),
                 dma((beams, 2)),
                 dma((beams, 2)),
             ],

time: 124 us -> 122 us (0.984)
  Pallas kernels: 122 us -> 120 us
    pallas_call x1, Pallas kernels: 122 us -> 120 us  [step(): pl.pallas_call(functools.partial(kernel, size), out_shape=jax.ShapeDtypeS...]
where the time goes in v3:
time: 122 us
  Pallas kernels  120 us (98%)
  local copies, waits for them, and re-layouts  1.87 us (2%)
    pallas_call x1, Pallas kernels, step(): pl.pallas_call(functools.partial(kernel, size), out_shape=jax.ShapeDtypeS...  120 us

profile of v3, /device:TPU:37, one launch (start us, length us, event | category | flops | bytes accessed | tf_op | source)
XLA Modules:
  0.0 121.9 jit_solution(7111135846357351041)
XLA Ops:
  0.0 120.0 %pulse_doppler.1 = f32[1,2,512,128]{3,2,1,0:T(8,128)} custom-call(f32[1,2,2,8,8192]{4,3,2,1,0:T(8,128)} %echoes.1, f32[2,8192]{1,0:T(2,128)} %waveform.1, f32[512]{0:T(512)} %taper.1, s32[2]{0:T(128)} %guard.1, s32[2]{0:T(128)} %train.1, f32[2]{0:T(128)} %noise.1, bf16[2,128,384]{2,1,0:T(8,128)(2,1)} %constant.6.clone.tab_a, ...), custom_call_target="tpu_custom_call" | custom-call | tf_op jit(solution)/shard_map/pulse_doppler/pallas_call | solution.py:473
  120.0 1.9 %copy.11 = f32[1,2,512,128]{3,2,1,0:T(8,128)} copy(f32[1,2,512,128]{3,2,1,0:T(8,128)} %pulse_doppler.1) | data formatting | bytes 1048576

commit v4 on v3

--- a/solution.py
+++ b/solution.py
@@ -472,7 +472,7 @@
         dma = pltpu.SemaphoreType.DMA
         return pl.pallas_call(
             functools.partial(kernel, size),
-            out_shape=jax.ShapeDtypeStruct((1, beams, depth, GB), F32),
+            out_shape=vmem((1, beams, depth, GB), F32),
             in_specs=[hbm, hbm, smem, smem, smem, smem, hbm, hbm, hbm],
             out_specs=pl.BlockSpec(memory_space=vmem),
             scratch_shapes=[

time: 122 us -> 120 us (0.984)
  no operation moved by 1% of the time
where the time goes in v4:
time: 120 us
  Pallas kernels  119 us (99%)
    pallas_call x1, Pallas kernels, step(): pl.pallas_call(functools.partial(kernel, size), out_shape=vmem((1, beams,...  119 us

profile of v4, /device:TPU:37, one launch (start us, length us, event | category | flops | bytes accessed | tf_op | source)
XLA Modules:
  0.0 120.0 jit_solution(7715236244293774299)
XLA Ops:
  0.0 119.2 %pulse_doppler.1 = f32[1,2,512,128]{3,2,1,0:T(8,128)S(1)} custom-call(f32[1,2,2,8,8192]{4,3,2,1,0:T(8,128)} %echoes.1, f32[2,8192]{1,0:T(2,128)} %waveform.1, f32[512]{0:T(512)} %taper.1, s32[2]{0:T(128)} %guard.1, s32[2]{0:T(128)} %train.1, f32[2]{0:T(128)} %noise.1, bf16[2,128,384]{2,1,0:T(8,128)(2,1)} %constant.6.clone.tab_a, ...), custom_call_target="tpu_custom_call" | custom-call | tf_op jit(solution)/shard_map/pulse_doppler/pallas_call | solution.py:473
  119.2 0.8 copy.11

commit v5 on v4

--- a/solution.py
+++ b/solution.py
@@ -15,6 +15,8 @@
 HALO = 20
 HOP = 8
 NEAR = 2
+PAUSE = 10
+HOLDERS = 24
 F32 = jnp.float32
 BF16 = jnp.bfloat16
 
@@ -207,6 +209,7 @@
     dop,
     power,
     window,
+    edge_band,
     halo_out,
     halo_in,
     in_sem,
@@ -308,7 +311,7 @@
             device_id_type=MESH,
         )
 
-    def start_by_place(b, lo, hi, to=None):
+    def start_by_place(b, lo, hi, to=None, hold=False):
         def both(offset):
             for k in range(2):
                 direct(b, at(offset, k)).start()
@@ -339,7 +342,10 @@
             if to != 1:
                 for place in range(half):
                     up = chips - chip + place
-                    when((up >= lo) & (up <= min(hi, half - 1)), up)
+                    inside = (up >= lo) & (up <= min(hi, half - 1))
+                    if hold and place >= PAUSE:
+                        inside &= chip < HOLDERS
+                    when(inside, up)
                     down = chip - place
                     when((down >= lo) & (down <= min(hi, half - 1)), -down)
             if to != 0:
@@ -350,6 +356,18 @@
 
         pl.when(first_half)(early)
         pl.when(jnp.logical_not(first_half))(late)
+
+    def start_held(b):
+        def both(offset):
+            for k in range(2):
+                direct(b, at(offset, k)).start()
+
+        def last():
+            for place in range(PAUSE, half):
+                up = chips - chip + place
+                pl.when(up < half)(lambda: both(up))
+
+        pl.when(chip >= HOLDERS)(last)
 
     def tell(step):
         for sign in (1, -1):
@@ -388,17 +406,21 @@
             pl.when(inner[side])(halo_copy(b, side).start)
 
     def cfar_inside(b):
+        own_band, left_band, right_band = bands(guard[b], train[b])
         high, low = split(power[b])
-        band = bands(guard[b], train[b])[0].astype(BF16)
+        band = own_band.astype(BF16)
         window[b] = jnp.dot(
             jnp.concatenate([high, low], axis=1),
             jnp.concatenate([band, band], axis=0),
             preferred_element_type=F32,
         )
+        slot = lax.div(lax.broadcasted_iota(jnp.int32, (GB, GB), 0), 32)
+        for r in range(4):
+            lb = jnp.where(slot == r, left_band, 0.0).astype(BF16)
+            rb = jnp.where(slot == r, right_band, 0.0).astype(BF16)
+            edge_band[b, r] = jnp.concatenate([lb, lb, rb, rb], axis=0)
 
     def cfar(b):
-        _, left_band, right_band = bands(guard[b], train[b])
-        slot = lax.div(lax.broadcasted_iota(jnp.int32, (GB, GB), 0), 32)
         rows = depth // 4
         for side in range(2):
 
@@ -418,11 +440,7 @@
         floor = noise[b]
         inverse = 1.0 / (2.0 * train[b].astype(F32))
         for r in range(4):
-            lb = jnp.where(slot == r, left_band, 0.0).astype(BF16)
-            rb = jnp.where(slot == r, right_band, 0.0).astype(BF16)
-            more = jnp.dot(
-                edges, jnp.concatenate([lb, lb, rb, rb], axis=0), preferred_element_type=F32
-            )
+            more = jnp.dot(edges, edge_band[b, r], preferred_element_type=F32)
             here = slice(r * rows, (r + 1) * rows)
             out[0, b, here, :] = power[b, here, :] / (floor + (window[b, here, :] + more) * inverse)
 
@@ -444,7 +462,7 @@
     start_by_place(0, HOP + 1, half)
     for b in range(1, beams):
         direct(b, partner).start()
-        start_by_place(b, 1, half)
+        start_by_place(b, 1, half, hold=True)
     for l in range(pulses):
         for i in range(2):
             col = i * pulses + l
@@ -453,6 +471,9 @@
         wait_blocks(recv_sem.at[b], size - 1)
         doppler(b)
         cfar_inside(b)
+        if b == 0:
+            for other in range(1, beams):
+                start_held(other)
     for b in range(beams):
         cfar(b)
     for b in range(beams):
@@ -489,6 +510,7 @@
                 vmem((2, GA, pulses * GB), F32),
                 vmem((beams, depth, GB), F32),
                 vmem((beams, depth, GB), F32),
+                vmem((beams, 4, 4 * GB, GB), BF16),
                 vmem((beams, 2, depth // 4, GB), F32),
                 vmem((beams, 2, depth // 4, GB), F32),
                 dma((4 + beams,)),

time: 120 us -> 120 us (level)
  no operation moved by 1% of the time
where the time goes in v5:
time: 120 us; the launch traced here: 119 us
  Pallas kernels  119 us (99%)
    pallas_call x1, Pallas kernels, step(): pl.pallas_call(functools.partial(kernel, size), out_shape=vmem((1, beams,...  119 us

profile of v5, /device:TPU:37, one launch (start us, length us, event | category | flops | bytes accessed | tf_op | source)
XLA Modules:
  0.0 119.4 jit_solution(1597512760527737168)
XLA Ops:
  0.0 118.6 %pulse_doppler.1 = f32[1,2,512,128]{3,2,1,0:T(8,128)S(1)} custom-call(f32[1,2,2,8,8192]{4,3,2,1,0:T(8,128)} %echoes.1, f32[2,8192]{1,0:T(2,128)} %waveform.1, f32[512]{0:T(512)} %taper.1, s32[2]{0:T(128)} %guard.1, s32[2]{0:T(128)} %train.1, f32[2]{0:T(128)} %noise.1, bf16[2,128,384]{2,1,0:T(8,128)(2,1)} %constant.6.clone.tab_a, ...), custom_call_target="tpu_custom_call" | custom-call | tf_op jit(solution)/shard_map/pulse_doppler/pallas_call | solution.py:494
  118.6 0.8 copy.11

commit v6 on v5

--- a/solution.py
+++ b/solution.py
@@ -241,11 +241,11 @@
         loads[name] = pltpu.make_async_copy(src, dst, in_sem.at[i])
         loads[name].start()
 
+    load("w", waveform, w_in, 4)
     load("x0", echoes.at[0, :, 0], x_in.at[0], 0)
     load("ta", tab_a, ta, 1)
     load("tw", twid, tw, 2)
     load("tb", tab_b, tb, 3)
-    load("w", waveform, w_in, 4)
     for b in range(1, beams):
         load(f"x{b}", echoes.at[0, :, b], x_in.at[b], 4 + b)
 
@@ -268,10 +268,6 @@
         greeters += jnp.where(lax.rem(chip + d + chips, chips) < half, 2, 0)
 
     def range_compress(b):
-        loads[f"x{b}"].wait()
-        for ri in range(2):
-            for j in range(GA):
-                x_rows[ri, j * pulses : (j + 1) * pulses, :] = x_in[b, ri, :, j * GB : (j + 1) * GB]
         if b == 0:
             loads["w"].wait()
             for ri in range(2):
@@ -280,6 +276,11 @@
             fr, fi = filter_grid(grid[...])
             filt[0] = fr
             filt[1] = fi
+        loads[f"x{b}"].wait()
+        for ri in range(2):
+            for j in range(GA):
+                x_rows[ri, j * pulses : (j + 1) * pulses, :] = x_in[b, ri, :, j * GB : (j + 1) * GB]
+        if b == 0:
             for name in ("ta", "tw", "tb"):
                 loads[name].wait()
         rows = [
@@ -295,6 +296,8 @@
                 own[b, ri, pl.ds(p, GA, stride=pulses), :] = (
                     done[ri * GA : (ri + 1) * GA, p * GB : (p + 1) * GB] * weight
                 )
+
+    def keep_own(b):
         mine = pl.ds(pl.multiple_of(me * pulses, pulses), pulses)
         recv[b, :, mine, :] = own[b, :, mine, :]
 
@@ -463,6 +466,8 @@
     for b in range(1, beams):
         direct(b, partner).start()
         start_by_place(b, 1, half, hold=True)
+    for b in range(beams):
+        keep_own(b)
     for l in range(pulses):
         for i in range(2):
             col = i * pulses + l

time: 120 us -> 120 us (level)
  no operation moved by 1% of the time
where the time goes in v6:
time: 120 us; the launch traced here: 119 us
  Pallas kernels  118 us (98%)
    pallas_call x1, Pallas kernels, step(): pl.pallas_call(functools.partial(kernel, size), out_shape=vmem((1, beams,...  118 us

profile of v6, /device:TPU:37, one launch (start us, length us, event | category | flops | bytes accessed | tf_op | source)
XLA Modules:
  0.0 119.2 jit_solution(12402662780830463589)
XLA Ops:
  0.0 118.4 %pulse_doppler.1 = f32[1,2,512,128]{3,2,1,0:T(8,128)S(1)} custom-call(f32[1,2,2,8,8192]{4,3,2,1,0:T(8,128)} %echoes.1, f32[2,8192]{1,0:T(2,128)} %waveform.1, f32[512]{0:T(512)} %taper.1, s32[2]{0:T(128)} %guard.1, s32[2]{0:T(128)} %train.1, f32[2]{0:T(128)} %noise.1, bf16[2,128,384]{2,1,0:T(8,128)(2,1)} %constant.6.clone.tab_a, ...), custom_call_target="tpu_custom_call" | custom-call | tf_op jit(solution)/shard_map/pulse_doppler/pallas_call | solution.py:499
  118.4 0.8 copy.11

commit v7 on v6

--- a/solution.py
+++ b/solution.py
@@ -15,8 +15,8 @@
 HALO = 20
 HOP = 8
 NEAR = 2
-PAUSE = 10
-HOLDERS = 24
+PAUSE = 9
+HOLDERS = 28
 F32 = jnp.float32
 BF16 = jnp.bfloat16
 

time: 120 us -> 119 us (level)
  no operation moved by 1% of the time
where the time goes in v7:
time: 119 us
  Pallas kernels  119 us (100%)
    pallas_call x1, Pallas kernels, step(): pl.pallas_call(functools.partial(kernel, size), out_shape=vmem((1, beams,...  119 us

profile of v7, /device:TPU:37, one launch (start us, length us, event | category | flops | bytes accessed | tf_op | source)
XLA Modules:
  0.0 119.3 jit_solution(14629803139138343634)
XLA Ops:
  0.0 118.5 %pulse_doppler.1 = f32[1,2,512,128]{3,2,1,0:T(8,128)S(1)} custom-call(f32[1,2,2,8,8192]{4,3,2,1,0:T(8,128)} %echoes.1, f32[2,8192]{1,0:T(2,128)} %waveform.1, f32[512]{0:T(512)} %taper.1, s32[2]{0:T(128)} %guard.1, s32[2]{0:T(128)} %train.1, f32[2]{0:T(128)} %noise.1, bf16[2,128,384]{2,1,0:T(8,128)(2,1)} %constant.6.clone.tab_a, ...), custom_call_target="tpu_custom_call" | custom-call | tf_op jit(solution)/shard_map/pulse_doppler/pallas_call | solution.py:499
  118.6 0.8 copy.11
